TPU v7x, 128 devices: a whole 4x4x4 slice. The times are simulated.
128 devices in a mesh: row: 16 (over z, x), col: 8 (over y, core).
Axes of the slice: x: 4, y: 4, z: 4, core: 2. Of those that a mesh axis runs over, the one named last changes fastest.
Arguments:
- pole_values: float32 [65536], P('row'), may hold values from -32768 to 32768, as said below
- weights: float32 [65536], P('row'), may hold values from 0.15 to 0.5
- centers: float32 [65536], P('col'), as said below
- offsets: float32 [65536], P('col'), may hold values from -0.1 to 0.1
- chosen: int32 [2048], replicated, may hold values from 0 to 65535
- column_pole: int32 [2, 32768], P(None, 'row'), may hold values from 0 to 65535, as said below
- eigen_blocks: bfloat16 [6144, 2, 32768], P('col', None, 'row'), may hold values from -6 to 6
Outputs:
- roots_offset: float32 [65536], P('col')
- panel: float32 [6144, 2, 2048], P(('col', 'row'))
Inputs may be any that keep to these rules, and one draw needn't show every extreme that they name: `pole_values`: ascending; consecutive poles differ by 1/4 to 7/4; every pole is a multiple of 1/128. centers[i] is the midpoint of pole_values[i] and pole_values[i + 1]; the last one is the last pole plus 1/2. `chosen`: indices of roots. `column_pole`: each of 0 to 65535 stands once.
All inputs are finite; a program needn't handle non-finite values.
Results may differ from a plain program's by a relative error of at most 0.0021.
Values may be sent and summed in bfloat16 or wider, within the bound.
A program may use at most 128 MiB of HBM per device.

v0:
```python
import jax
import jax.numpy as jnp
from jax import lax
from jax.sharding import Mesh
from jax.sharding import PartitionSpec as P

ITERS = 3
ROW = ("row_0", "row_1")
COL_ROW = ("col", "row_0", "row_1")


def gather_turned(arrays, axis, dims):
    turned = [jnp.moveaxis(a, dim, 0) for a, dim in zip(arrays, dims)]
    widths = [t[0].size for t in turned]
    both = jnp.concatenate([t.reshape(-1, w) for t, w in zip(turned, widths)], axis=1)
    filled = lax.all_gather(both, axis, axis=0, tiled=True)
    blocks = jnp.split(filled, [sum(widths[:k]) for k in range(1, len(widths))], axis=1)
    return tuple(
        (
            jnp.moveaxis(b.reshape(-1, *t.shape[1:]), 0, dim)
            for b, t, dim in zip(blocks, turned, dims)
        )
    )


def copy_for_each(shard, axis):
    size = lax.axis_size(axis)
    return lax.all_to_all(
        jnp.broadcast_to(shard[None], (size, *shard.shape)), axis, 0, 0, tiled=True
    )


def joined_along(blocks, dim):
    blocks = jnp.moveaxis(blocks, 0, dim)
    lengths = blocks.shape
    return blocks.reshape(*lengths[:dim], lengths[dim] * lengths[dim + 1], *lengths[dim + 2 :])


def gather_directly(shard, axis, dim):
    blocks = copy_for_each(shard, axis)
    return joined_along(blocks, dim)


def by_axis(shard, axes):
    for axis in axes:
        shard = lax.psum(shard, axis)
    return shard


def block_sums(pole_vals, weight_sq, center_vals, offset_vals, block_rows):
    root_count = center_vals.shape[0]
    block_rows = min(block_rows, root_count)
    center_blocks = center_vals.reshape(root_count // block_rows, block_rows)
    offset_blocks = offset_vals.reshape(root_count // block_rows, block_rows)

    def per_block(blocks):
        distance = pole_vals[None, :] - blocks[0][:, None] - blocks[1][:, None]
        inverse = 1.0 / distance
        weighted = weight_sq[None, :] * inverse
        return (
            jnp.sum(weighted, axis=1),
            jnp.sum(weighted * inverse, axis=1),
            jnp.min(jnp.abs(distance), axis=1),
        )

    sums = lax.map(per_block, (center_blocks, offset_blocks))
    return tuple((item.reshape(root_count) for item in sums))


def newton_update(offset_now, sum_inverse, sum_square, nearest):
    limit = 0.5 * nearest
    return offset_now - jnp.clip((1.0 + sum_inverse) / sum_square, -limit, limit)


def cauchy_block(pole_picked, weight_picked, panel_center, panel_offset, inv_norm):
    distance = pole_picked[:, None] - panel_center[None, :] - panel_offset[None, :]
    return (weight_picked[:, None] * (1.0 / distance) * inv_norm[None, :]).astype(jnp.bfloat16)


def on_device(pole_values, weights, centers, offsets, chosen, column_pole, eigen_blocks):
    all_poles, all_weights = gather_turned((pole_values, weights), ROW, (0, 0))
    weight_sq = weights * weights
    per_device = offsets.shape[0] // lax.axis_size(ROW)
    first_root = lax.axis_index(ROW) * per_device
    my_centers = lax.dynamic_slice_in_dim(centers, first_root, per_device)
    my_offsets = lax.dynamic_slice_in_dim(offsets, first_root, per_device)
    all_sq = all_weights * all_weights
    for iteration in range(ITERS):
        sum_inverse, sum_square, nearest = block_sums(all_poles, all_sq, my_centers, my_offsets, 32)
        my_offsets = newton_update(my_offsets, sum_inverse, sum_square, nearest)
    offset_now = gather_directly(my_offsets, ROW, 0)
    full_centers, full_offsets = gather_turned((centers, offset_now), "col", (0, 0))
    panel_center = full_centers[chosen]
    panel_offset = full_offsets[chosen]
    partial_sq = block_sums(pole_values, weight_sq, panel_center, panel_offset, 64)[1]
    norm_sq = by_axis(partial_sq, ROW)
    inv_norm = lax.rsqrt(norm_sq)
    cauchy_halves = []
    for half_index in range(2):
        pole_index = column_pole[half_index]
        cauchy_halves.append(
            cauchy_block(
                all_poles[pole_index], all_weights[pole_index], panel_center, panel_offset, inv_norm
            )
        )
    panel = lax.psum_scatter(
        jnp.stack(
            [
                jnp.dot(
                    eigen_blocks[:, half_index, :],
                    cauchy_halves[half_index],
                    preferred_element_type=jnp.float32,
                )
                for half_index in range(2)
            ],
            axis=1,
        ),
        ROW,
        scatter_dimension=0,
        tiled=True,
    )
    return (offset_now, panel)


def solution(mesh):
    torus = Mesh(mesh.devices.reshape(4, 4, mesh.shape["col"]), ("row_0", "row_1", "col"))
    placed = (P(ROW), P(ROW), P("col"), P("col"), P(), P(None, ROW), P("col", None, ROW))
    return jax.shard_map(
        on_device,
        mesh=torus,
        in_specs=placed,
        out_specs=(P("col"), P(COL_ROW, None, None)),
        check_vma=False,
    )
```

profile of v0, /device:TPU:1, one launch (start us, length us, event | category | flops | bytes accessed | tf_op | source)
XLA Modules:
  0.0 557.3 jit_solution(9556216317746386524)
XLA Ops:
  9.6 21.0 %all_gather.6 = f32[65536,2]{0,1:T(2,128)S(1)} all-gather(f32[4096,2]{0,1:T(2,128)S(1)} %pad_maximum_fusion.2), channel_id=1, replica_groups=mesh['row_0'=4,'row_1'=4,'col'=8] {'row_0','row_1'}, dimensions={0}, use_global_device_ids=true | all-gather | bytes 557056 | tf_op jit(solution)/shard_map/all_gather | solution.py:16
  31.1 46.1 %while.52 = (s32[]{:T(128)}, f32[16,32]{1,0:T(8,128)S(1)}, f32[16,32]{1,0:T(8,128)S(1)}, f32[16,32]{1,0:T(8,128)S(1)}, f32[65536]{0:T(1024)S(1)}, /*index=5*/f32...) while((s32[]{:T(128)}, f32[16,32]{1,0:T(8,128)S(1)}, ...), condition=%wide.region_4.5_spmd, body=%wide.region_0.4_spmd.sunk | while | flops 18874272 | bytes 526325 | solution.py:66
  31.1 2.7 fusion.33
  34.0 2.7 fusion.33
  36.9 2.7 fusion.33
  39.8 2.7 fusion.33
  42.7 2.7 fusion.33
  45.5 2.7 fusion.33
  48.4 2.7 fusion.33
  51.3 2.7 fusion.33
  54.2 2.7 fusion.33
  57.0 2.7 fusion.33
  59.9 2.7 fusion.33
  62.8 2.7 fusion.33
  65.7 2.7 fusion.33
  68.6 2.7 fusion.33
  71.4 2.7 fusion.33
  74.3 2.7 fusion.33
  78.2 46.1 %while.53 = (s32[]{:T(128)}, f32[16,32]{1,0:T(8,128)S(1)}, f32[16,32]{1,0:T(8,128)S(1)}, f32[16,32]{1,0:T(8,128)S(1)}, f32[65536]{0:T(1024)S(1)}, /*index=5*/f32...) while((s32[]{:T(128)}, f32[16,32]{1,0:T(8,128)S(1)}, ...), condition=%wide.region_9.10_spmd, body=%wide.region_5.9_spmd.sunk | while | flops 18874272 | bytes 526325 | solution.py:66
  78.2 2.7 fusion.34
  81.1 2.7 fusion.34
  84.0 2.7 fusion.34
  86.9 2.7 fusion.34
  89.7 2.7 fusion.34
  92.6 2.7 fusion.34
  95.5 2.7 fusion.34
  98.4 2.7 fusion.34
  101.3 2.7 fusion.34
  104.1 2.7 fusion.34
  124.5 46.1 %while.54 = (s32[]{:T(128)}, f32[16,32]{1,0:T(8,128)S(1)}, f32[16,32]{1,0:T(8,128)S(1)}, f32[16,32]{1,0:T(8,128)S(1)}, f32[65536]{0:T(1024)S(1)}, /*index=5*/f32...) while((s32[]{:T(128)}, f32[16,32]{1,0:T(8,128)S(1)}, ...), condition=%wide.region_14.15_spmd, body=%wide.region_10.14_spmd.sunk | while | flops 18874272 | bytes 526325 | solution.py:66
  159.1 2.7 fusion.35
  171.4 4.7 all-to-all-start
  176.2 13.8 %fusion.26 = (bf16[768,1,2048]{2,1,0:T(2,128)(2,1)}, bf16[768,1,2048]{2,1,0:T(2,128)(2,1)}) fusion(bf16[768,2,2048]{2,1,0:T(2,128)(2,1)} %param.21), kind=kLoop, calls=%fused_computation.75 | loop fusion | bytes 12582912 | tf_op jit(solution)/shard_map/slice | solution.py:110
  190.1 11.8 %gather_fusion = f32[2048]{0:T(1024)S(1)} fusion(f32[65536]{0:T(1024)S(1)} %bitcast.100, s32[2048]{0:T(1024)S(1)} %broadcast_clamp_fusion.1), kind=kCustom, calls=%fused_computation | custom fusion | bytes 24576 | tf_op jit(solution)/shard_map/gather | solution.py:103
  201.9 11.8 %gather_fusion.1 = f32[2048]{0:T(1024)S(1)} fusion(f32[65536]{0:T(1024)S(1)} %bitcast.96, s32[2048]{0:T(1024)S(1)} %broadcast_clamp_fusion.1), kind=kCustom, calls=%fused_computation.1 | custom fusion | bytes 24576 | tf_op jit(solution)/shard_map/gather | solution.py:103
  213.7 11.8 %gather_fusion.5 = f32[2048]{0:T(1024)S(1)} fusion(f32[65536]{0:T(1024)S(1)} %bitcast.97, s32[2048]{0:T(1024)S(1)} %broadcast_clamp_fusion), kind=kCustom, calls=%fused_computation.5 | custom fusion | bytes 24576 | tf_op jit(solution)/shard_map/gather | solution.py:103
  225.5 11.8 %gather_fusion.4 = f32[2048]{0:T(1024)S(1)} fusion(f32[65536]{0:T(1024)S(1)} %bitcast.101, s32[2048]{0:T(1024)S(1)} %broadcast_clamp_fusion), kind=kCustom, calls=%fused_computation.4 | custom fusion | bytes 24576 | tf_op jit(solution)/shard_map/gather | solution.py:103
  237.4 19.6 %all_gather.7 = f32[65536,2]{0,1:T(2,128)S(1)} all-gather(f32[8192,2]{0,1:T(2,128)S(1)} %pad_maximum_fusion.1), channel_id=1, replica_groups=mesh['row_0'=4,'row_1'=4,'col'=8] {'col'}, dimensions={0}, use_global_device_ids=true | all-gather | bytes 589824 | tf_op jit(solution)/shard_map/all_gather | solution.py:16
  257.4 11.8 %gather_fusion.2 = f32[2048]{0:T(1024)S(1)} fusion(f32[65536]{0:T(1024)S(1)} %bitcast.103, s32[2048]{0:T(1024)S(1)} %fusion.23), kind=kCustom, calls=%fused_computation.2 | custom fusion | bytes 24576 | tf_op jit(solution)/shard_map/gather | solution.py:93
  269.3 11.8 %gather_fusion.3 = f32[2048]{0:T(1024)S(1)} fusion(f32[65536]{0:T(1024)S(1)} %bitcast.102, s32[2048]{0:T(1024)S(1)} %fusion.23), kind=kCustom, calls=%fused_computation.3 | custom fusion | bytes 24576 | tf_op jit(solution)/shard_map/gather | solution.py:94
  281.1 14.2 %while.55 = (s32[]{:T(128)}, f32[32,64]{1,0:T(8,128)S(1)}, f32[4096]{0:T(1024)S(1)}, f32[4096]{0:T(1024)S(1)}, f32[32,64]{1,0:T(8,128)S(1)}, /*index=5*/f32[32,64]{1,0:T(8,128)S(1)}, s32[]{:T(128)}, s32[]{:T(128)}) while((s32[]{:T(128)}, f32[32,64]{1,0:T(8,128)S(1)}, f32[4096]{0:T(1024)S(1)}, f32[4096]{0:T(1024)S(1)}, ...), condition=%wide.region_17.18_spmd, body=%wide.region_15.17_spmd.sunk | while | flops 1572802 | bytes 35165 | solution.py:66
  295.4 8.9 %psum.14 = f32[2048]{0:T(1024)S(1)} all-reduce(f32[2048]{0:T(1024)S(1)} %reshape.184), channel_id=1, replica_groups=mesh['row_0'=4,'row_1'=4,'col'=8] {'row_0'}, use_global_device_ids=true, to_apply=%region_18.19 | all-reduce | flops 2048 | bytes 16384 | tf_op jit(solution)/shard_map/psum | solution.py:46
  304.3 8.7 %psum.15 = f32[2048]{0:T(1024)S(1)} all-reduce(f32[2048]{0:T(1024)S(1)} %psum.14), channel_id=1, replica_groups=mesh['row_0'=4,'row_1'=4,'col'=8] {'row_1'}, use_global_device_ids=true, to_apply=%region_19.20 | all-reduce | flops 2048 | bytes 16384 | tf_op jit(solution)/shard_map/psum | solution.py:46
  313.0 14.9 %fusion.22 = f32[768,1,2048]{0,2,1:T(8,128)} fusion(f32[2048]{0:T(1024)S(1)} %rsqrt.3, f32[2048]{0:T(1024)S(1)} %gather_fusion.3, f32[2048]{0:T(1024)S(1)} %gather_fusion.2, f32[2048]{0:T(1024)S(1)} %gather_fusion.1, f32[2048]{0:T(1024)S(1)} %gather_fusion, bf16[768,1,2048]{2,1,0:T(2,128)(2,1)} %get-tuple-element.257), kind=kOutput, calls=%fused_computation.52 | convolution fusion | flops 6467616768 | bytes 9478144 | tf_op jit(solution)/shard_map/dot_general | solution.py:109
  327.9 12.2 %fusion.21 = f32[768,1,2048]{0,2,1:T(8,128)} fusion(f32[2048]{0:T(1024)S(1)} %gather_fusion.5, f32[2048]{0:T(1024)S(1)} %gather_fusion.4, f32[2048]{0:T(1024)S(1)} %rsqrt.3, f32[2048]{0:T(1024)S(1)} %gather_fusion.3, f32[2048]{0:T(1024)S(1)} %gather_fusion.2, bf16[768,1,2048]{2,1,0:T(2,128)(2,1)S(1)} %bitcast.105), kind=kOutput, calls=%fused_computation.51 | convolution fusion | flops 6467616768 | bytes 9478144 | tf_op jit(solution)/shard_map/dot_general | solution.py:109
  340.1 10.0 %pad_maximum_fusion = f32[768,2,2048]{0,2,1:T(8,128)} fusion(f32[768,1,2048]{0,2,1:T(8,128)} %fusion.21, f32[768,1,2048]{0,2,1:T(8,128)} %fusion.22), kind=kLoop, calls=%fused_computation.36 | loop fusion | flops 3145728 | bytes 25165824 | tf_op jit(solution)/shard_map/stack | solution.py:107
  350.1 19.4 %copy.18 = f32[768,2,2048]{2,1,0:T(2,128)} copy(f32[768,2,2048]{0,2,1:T(8,128)} %pad_maximum_fusion) | data formatting | bytes 25165824 | tf_op jit(solution)/shard_map/stack | solution.py:107
  371.4 176.4 %all-reduce.3.cloned.1.call-done = f32[768,2,2048]{2,1,0:T(2,128)} async-done(((f32[768,2,2048]{2,1,0:T(2,128)}), f32[768,2,2048]{2,1,0:T(2,128)}) %all-reduce.3.cloned.1.call-update) | async-done | bytes 12582928
  (377 shorter events, 86.3 us)
Async XLA Ops:
  7.2 169.0 %copy-start.4 = (s32[2048]{0:T(1024)S(1)}, s32[2048]{0:T(1024)}, u32[]{:S(2)}) copy-start(s32[2048]{0:T(1024)} %param.19) | copy-start | bytes 24580
  7.2 169.0 %copy-start.3 = (s32[2,2048]{1,0:T(2,128)S(1)}, s32[2,2048]{1,0:T(2,128)}, u32[]{:S(2)}) copy-start(s32[2,2048]{1,0:T(2,128)} %param.20) | copy-start | bytes 49156
  171.4 65.9 %all-to-all-start = ((f32[16,1,512]{2,1,0:T(1,128)}), f32[16,1,512]{2,1,0:T(1,128)S(1)}, u32[]{:S(2)}, u32[]{:S(2)}) async-start(f32[16,1,512]{2,1,0:T(1,128)} %broadcast_in_dim.72), calls=%async_computation | async-start | bytes 65536 | tf_op jit(solution)/shard_map/all_to_all | solution.py:28
  176.1 371.7 %all-reduce.3.cloned.1.call-start = ((), (), s32[]{:S(2)}) async-start(), calls=%async_computation.1 | async-start | bytes 25165824
  176.2 13.9 %copy-start.1 = (f32[4096]{0:T(1024)S(1)}, f32[4096]{0:T(1024)}, u32[]{:S(2)}) copy-start(f32[4096]{0:T(1024)} %param.16) | copy-start | bytes 49156
  213.7 23.6 %copy-start.2 = (f32[8192]{0:T(1024)S(1)}, f32[8192]{0:T(1024)}, u32[]{:S(2)}) copy-start(f32[8192]{0:T(1024)} %param.17) | copy-start | bytes 98308
  257.4 23.7 %copy-start = (f32[4096]{0:T(1024)S(1)}, f32[4096]{0:T(1024)}, u32[]{:S(2)}) copy-start(f32[4096]{0:T(1024)} %param.15) | copy-start | bytes 49156
  269.3 58.6 %slice-start = ((s8[6291456]{0:T(1024)(128)(4,1)}), s8[2097152]{0:T(1024)(128)(4,1)S(1)}, s32[]{:S(2)}) async-start(s8[6291456]{0:T(1024)(128)(4,1)} %bitcast.104), calls=%async_computation.2 | async-start | bytes 4194304
  313.0 14.9 %slice-start.1 = ((s8[6291456]{0:T(1024)(128)(4,1)}), s8[4194304]{0:T(1024)(128)(4,1)S(1)}, s32[]{:S(2)}) async-start(s8[6291456]{0:T(1024)(128)(4,1)} %bitcast.104), calls=%async_computation.3 | async-start | bytes 8388608
  369.5 0.7 copy-start.5
Sparse Core Ops, SparseCore 0:
  369.6 178.0 all-reduce.2
where the time goes:
time: 558 us; the launch traced here: 557 us
  waiting for transfers between devices  176 us (32%)
  other arithmetic  155 us (28%)
  local copies, waits for them, and re-layouts  119 us (21%)
  blocking collectives  58.2 us (10%)
  matrix products  27 us (5%)
  between operations  15 us (3%)
    unnamed x2, waiting for transfers between devices  176 us
    reduce_sum x80, other arithmetic, per_block(): jnp.sum(weighted * inverse, axis=1)  143 us
    all_gather x2, blocking collectives, gather_turned(): filled = lax.all_gather(both, axis, axis=0, tiled=True)  40.6 us
    dot_general x2, matrix products, on_device(): jnp.dot(eigen_blocks[:, half_index, :], cauchy_halves[half_index], prefer...  27 us
    gather x2, local copies, waits for them, and re-layouts, on_device(): all_weights[pole_index]  23.6 us
    gather x2, local copies, waits for them, and re-layouts, on_device(): all_poles[pole_index]  23.6 us
    another operation x1, local copies, waits for them, and re-layouts, on_device(): jnp.stack([jnp.dot(eigen_blocks[:, half_index, :], cauchy_halves[half_ind...  19.4 us
    psum x2, blocking collectives, by_axis(): shard = lax.psum(shard, axis)  17.6 us
  transfers between devices with their start and end apart: 2, of which 1 were waited for; matrix products, arithmetic and copies ran while one was open for 11% of the time, Pallas kernels for 0%

commit v1 on v0

--- a/solution.py
+++ b/solution.py
@@ -13,7 +13,10 @@
     turned = [jnp.moveaxis(a, dim, 0) for a, dim in zip(arrays, dims)]
     widths = [t[0].size for t in turned]
     both = jnp.concatenate([t.reshape(-1, w) for t, w in zip(turned, widths)], axis=1)
-    filled = lax.all_gather(both, axis, axis=0, tiled=True)
+    peers = lax.axis_size(axis)
+    pieces = jnp.stack([both for _ in range(peers)])
+    pieces = lax.all_to_all(pieces, axis, split_axis=0, concat_axis=0)
+    filled = jnp.concatenate(pieces, axis=0)
     blocks = jnp.split(filled, [sum(widths[:k]) for k in range(1, len(widths))], axis=1)
     return tuple(
         (

time: 558 us -> 540 us (0.968)
  blocking collectives: 58.2 us -> 14.2 us
  starting transfers between devices: 4.71 us -> 22.2 us
  waiting for transfers between devices: 176 us -> 184 us
    all_gather x2 -> x0, blocking collectives: 40.6 us -> none  [gather_turned(): filled = lax.all_gather(both, axis, axis=0, tiled=True)]
    all_to_all x0 -> x2, starting transfers between devices: none -> 15.5 us  [gather_turned(): pieces = lax.all_to_all(pieces, axis, split_axis=0, concat_axis=0)]
    all_to_all x1, waiting for transfers between devices: 0.01 us -> 6.41 us  [copy_for_each(): lax.all_to_all(jnp.broadcast_to(shard[None], (size, *shard.shape)), axis,...]
  transfers between devices with their start and end apart: 2 -> 4, of which waited for: 1 -> 2; matrix products, arithmetic and copies ran while one was open for 11% -> 12% of each run, Pallas kernels for 0% -> 0%
where the time goes in v1:
time: 540 us; the launch traced here: 539 us
  waiting for transfers between devices  184 us (34%)
  other arithmetic  155 us (29%)
  local copies, waits for them, and re-layouts  120 us (22%)
  matrix products  27 us (5%)
  starting transfers between devices  22.2 us (4%)
  between operations  15 us (3%)
  blocking collectives  14.2 us (3%)
    unnamed x2, waiting for transfers between devices  177 us
    reduce_sum x80, other arithmetic, per_block(): jnp.sum(weighted * inverse, axis=1)  143 us
    dot_general x2, matrix products, on_device(): jnp.dot(eigen_blocks[:, half_index, :], cauchy_halves[half_index], prefer...  27 us
    gather x2, local copies, waits for them, and re-layouts, on_device(): all_weights[pole_index]  23.6 us
    gather x2, local copies, waits for them, and re-layouts, on_device(): all_poles[pole_index]  23.6 us
    another operation x1, local copies, waits for them, and re-layouts, on_device(): jnp.stack([jnp.dot(eigen_blocks[:, half_index, :], cauchy_halves[half_ind...  19.4 us
    all_to_all x2, starting transfers between devices, gather_turned(): pieces = lax.all_to_all(pieces, axis, split_axis=0, concat_axis=0)  15.5 us
    psum x2, blocking collectives, by_axis(): shard = lax.psum(shard, axis)  14.2 us
  transfers between devices with their start and end apart: 4, of which 2 were waited for; matrix products, arithmetic and copies ran while one was open for 12% of the time, Pallas kernels for 0%

profile of v1, /device:TPU:1, one launch (start us, length us, event | category | flops | bytes accessed | tf_op | source)
XLA Modules:
  0.0 539.3 jit_solution(7366753288016299267)
XLA Ops:
  8.9 8.4 %all-to-all-start = ((f32[16,4096,2]{1,2,0:T(2,128)}), f32[16,4096,2]{1,2,0:T(2,128)S(1)}, u32[]{:S(2)}, u32[]{:S(2)}) async-start(f32[16,4096,2]{1,2,0:T(2,128)} %stack.10), calls=%async_computation | async-start | bytes 1048576 | tf_op jit(solution)/shard_map/all_to_all | solution.py:18
  17.4 13.8 %fusion.26 = (bf16[768,1,2048]{2,1,0:T(2,128)(2,1)}, bf16[768,1,2048]{2,1,0:T(2,128)(2,1)}) fusion(bf16[768,2,2048]{2,1,0:T(2,128)(2,1)} %param.21), kind=kLoop, calls=%fused_computation.75 | loop fusion | bytes 12582912 | tf_op jit(solution)/shard_map/slice | solution.py:113
  32.7 46.1 %while.52 = (s32[]{:T(128)}, f32[16,32]{1,0:T(8,128)S(1)}, f32[16,32]{1,0:T(8,128)S(1)}, f32[16,32]{1,0:T(8,128)S(1)}, f32[65536]{0:T(1024)S(1)}, /*index=5*/f32...) while((s32[]{:T(128)}, f32[16,32]{1,0:T(8,128)S(1)}, ...), condition=%wide.region_4.5_spmd, body=%wide.region_0.4_spmd.sunk | while | flops 18874272 | bytes 526325 | solution.py:69
  32.8 2.7 fusion.33
  35.6 2.7 fusion.33
  38.5 2.7 fusion.33
  41.4 2.7 fusion.33
  44.3 2.7 fusion.33
  47.2 2.7 fusion.33
  50.0 2.7 fusion.33
  52.9 2.7 fusion.33
  55.8 2.7 fusion.33
  58.7 2.7 fusion.33
  61.5 2.7 fusion.33
  64.4 2.7 fusion.33
  67.3 2.7 fusion.33
  70.2 2.7 fusion.33
  73.1 2.7 fusion.33
  75.9 2.7 fusion.33
  79.8 46.1 %while.53 = (s32[]{:T(128)}, f32[16,32]{1,0:T(8,128)S(1)}, f32[16,32]{1,0:T(8,128)S(1)}, f32[16,32]{1,0:T(8,128)S(1)}, f32[65536]{0:T(1024)S(1)}, /*index=5*/f32...) while((s32[]{:T(128)}, f32[16,32]{1,0:T(8,128)S(1)}, ...), condition=%wide.region_9.10_spmd, body=%wide.region_5.9_spmd.sunk | while | flops 18874272 | bytes 526325 | solution.py:69
  79.8 2.7 fusion.34
  82.7 2.7 fusion.34
  85.6 2.7 fusion.34
  88.5 2.7 fusion.34
  91.4 2.7 fusion.34
  94.2 2.7 fusion.34
  97.1 2.7 fusion.34
  100.0 2.7 fusion.34
  102.9 2.7 fusion.34
  126.2 46.1 %while.54 = (s32[]{:T(128)}, f32[16,32]{1,0:T(8,128)S(1)}, f32[16,32]{1,0:T(8,128)S(1)}, f32[16,32]{1,0:T(8,128)S(1)}, f32[65536]{0:T(1024)S(1)}, /*index=5*/f32...) while((s32[]{:T(128)}, f32[16,32]{1,0:T(8,128)S(1)}, ...), condition=%wide.region_14.15_spmd, body=%wide.region_10.14_spmd.sunk | while | flops 18874272 | bytes 526325 | solution.py:69
  169.4 2.7 fusion.35
  173.0 6.7 %all-to-all-start.1 = ((f32[16,1,512]{2,1,0:T(1,128)}), f32[16,1,512]{2,1,0:T(1,128)S(1)}, u32[]{:S(2)}, u32[]{:S(2)}) async-start(f32[16,1,512]{2,1,0:T(1,128)} %broadcast_in_dim.72), calls=%async_computation.1 | async-start | bytes 65536 | tf_op jit(solution)/shard_map/all_to_all | solution.py:31
  179.7 6.4 %all-to-all-done.1 = f32[16,1,512]{2,1,0:T(1,128)S(1)} async-done(((f32[16,1,512]{2,1,0:T(1,128)}), f32[16,1,512]{2,1,0:T(1,128)S(1)}, u32[]{:S(2)}, u32[]{:S(2)}) %all-to-all-start.1) | async-done | bytes 32800 | tf_op jit(solution)/shard_map/all_to_all | solution.py:31
  187.2 7.1 %all-to-all-start.2 = ((f32[8,8192,2]{1,2,0:T(2,128)}), f32[8,8192,2]{1,2,0:T(2,128)S(1)}, u32[]{:S(2)}, u32[]{:S(2)}) async-start(f32[8,8192,2]{1,2,0:T(2,128)} %stack.11), calls=%async_computation.2 | async-start | bytes 1048576 | tf_op jit(solution)/shard_map/all_to_all | solution.py:18
  194.4 11.8 %gather_fusion = f32[2048]{0:T(1024)S(1)} fusion(f32[65536]{0:T(1024)S(1)} %bitcast.102, s32[2048]{0:T(1024)S(1)} %broadcast_clamp_fusion.1), kind=kCustom, calls=%fused_computation | custom fusion | bytes 24576 | tf_op jit(solution)/shard_map/gather | solution.py:106
  206.2 11.8 %gather_fusion.1 = f32[2048]{0:T(1024)S(1)} fusion(f32[65536]{0:T(1024)S(1)} %bitcast.98, s32[2048]{0:T(1024)S(1)} %broadcast_clamp_fusion.1), kind=kCustom, calls=%fused_computation.1 | custom fusion | bytes 24576 | tf_op jit(solution)/shard_map/gather | solution.py:106
  217.9 11.8 %gather_fusion.5 = f32[2048]{0:T(1024)S(1)} fusion(f32[65536]{0:T(1024)S(1)} %bitcast.99, s32[2048]{0:T(1024)S(1)} %broadcast_clamp_fusion), kind=kCustom, calls=%fused_computation.5 | custom fusion | bytes 24576 | tf_op jit(solution)/shard_map/gather | solution.py:106
  229.7 11.8 %gather_fusion.4 = f32[2048]{0:T(1024)S(1)} fusion(f32[65536]{0:T(1024)S(1)} %bitcast.103, s32[2048]{0:T(1024)S(1)} %broadcast_clamp_fusion), kind=kCustom, calls=%fused_computation.4 | custom fusion | bytes 24576 | tf_op jit(solution)/shard_map/gather | solution.py:106
  242.0 11.8 %gather_fusion.2 = f32[2048]{0:T(1024)S(1)} fusion(f32[65536]{0:T(1024)S(1)} %bitcast.105, s32[2048]{0:T(1024)S(1)} %fusion.23), kind=kCustom, calls=%fused_computation.2 | custom fusion | bytes 24576 | tf_op jit(solution)/shard_map/gather | solution.py:96
  253.8 11.8 %gather_fusion.3 = f32[2048]{0:T(1024)S(1)} fusion(f32[65536]{0:T(1024)S(1)} %bitcast.104, s32[2048]{0:T(1024)S(1)} %fusion.23), kind=kCustom, calls=%fused_computation.3 | custom fusion | bytes 24576 | tf_op jit(solution)/shard_map/gather | solution.py:97
  265.7 14.2 %while.55 = (s32[]{:T(128)}, f32[32,64]{1,0:T(8,128)S(1)}, f32[4096]{0:T(1024)S(1)}, f32[4096]{0:T(1024)S(1)}, f32[32,64]{1,0:T(8,128)S(1)}, /*index=5*/f32[32,64]{1,0:T(8,128)S(1)}, s32[]{:T(128)}, s32[]{:T(128)}) while((s32[]{:T(128)}, f32[32,64]{1,0:T(8,128)S(1)}, f32[4096]{0:T(1024)S(1)}, f32[4096]{0:T(1024)S(1)}, ...), condition=%wide.region_17.18_spmd, body=%wide.region_15.17_spmd.sunk | while | flops 1572802 | bytes 35165 | solution.py:69
  279.9 7.0 %psum.14 = f32[2048]{0:T(1024)S(1)} all-reduce(f32[2048]{0:T(1024)S(1)} %reshape.196), channel_id=1, replica_groups=mesh['row_0'=4,'row_1'=4,'col'=8] {'row_0'}, use_global_device_ids=true, to_apply=%region_18.19 | all-reduce | flops 2048 | bytes 16384 | tf_op jit(solution)/shard_map/psum | solution.py:49
  286.9 7.2 %psum.15 = f32[2048]{0:T(1024)S(1)} all-reduce(f32[2048]{0:T(1024)S(1)} %psum.14), channel_id=1, replica_groups=mesh['row_0'=4,'row_1'=4,'col'=8] {'row_1'}, use_global_device_ids=true, to_apply=%region_19.20 | all-reduce | flops 2048 | bytes 16384 | tf_op jit(solution)/shard_map/psum | solution.py:49
  294.1 14.8 %fusion.22 = f32[768,1,2048]{0,2,1:T(8,128)} fusion(f32[2048]{0:T(1024)S(1)} %rsqrt.3, f32[2048]{0:T(1024)S(1)} %gather_fusion.3, f32[2048]{0:T(1024)S(1)} %gather_fusion.2, f32[2048]{0:T(1024)S(1)} %gather_fusion.1, f32[2048]{0:T(1024)S(1)} %gather_fusion, bf16[768,1,2048]{2,1,0:T(2,128)(2,1)} %get-tuple-element.257), kind=kOutput, calls=%fused_computation.52 | convolution fusion | flops 6467616768 | bytes 9478144 | tf_op jit(solution)/shard_map/dot_general | solution.py:112
  309.0 12.2 %fusion.21 = f32[768,1,2048]{0,2,1:T(8,128)} fusion(f32[2048]{0:T(1024)S(1)} %gather_fusion.5, f32[2048]{0:T(1024)S(1)} %gather_fusion.4, f32[2048]{0:T(1024)S(1)} %rsqrt.3, f32[2048]{0:T(1024)S(1)} %gather_fusion.3, f32[2048]{0:T(1024)S(1)} %gather_fusion.2, bf16[768,1,2048]{2,1,0:T(2,128)(2,1)S(1)} %bitcast.107), kind=kOutput, calls=%fused_computation.51 | convolution fusion | flops 6467616768 | bytes 9478144 | tf_op jit(solution)/shard_map/dot_general | solution.py:112
  321.2 10.0 %pad_maximum_fusion = f32[768,2,2048]{0,2,1:T(8,128)} fusion(f32[768,1,2048]{0,2,1:T(8,128)} %fusion.21, f32[768,1,2048]{0,2,1:T(8,128)} %fusion.22), kind=kLoop, calls=%fused_computation.36 | loop fusion | flops 3145728 | bytes 25165824 | tf_op jit(solution)/shard_map/stack | solution.py:110
  331.1 19.4 %copy.19 = f32[768,2,2048]{2,1,0:T(2,128)} copy(f32[768,2,2048]{0,2,1:T(8,128)} %pad_maximum_fusion) | data formatting | bytes 25165824 | tf_op jit(solution)/shard_map/stack | solution.py:110
  352.5 177.3 %all-reduce.3.cloned.1.call-done = f32[768,2,2048]{2,1,0:T(2,128)} async-done(((f32[768,2,2048]{2,1,0:T(2,128)}), f32[768,2,2048]{2,1,0:T(2,128)}) %all-reduce.3.cloned.1.call-update) | async-done | bytes 12582928
  (381 shorter events, 90.2 us)
Async XLA Ops:
  8.9 23.3 %all-to-all-start = ((f32[16,4096,2]{1,2,0:T(2,128)}), f32[16,4096,2]{1,2,0:T(2,128)S(1)}, u32[]{:S(2)}, u32[]{:S(2)}) async-start(f32[16,4096,2]{1,2,0:T(2,128)} %stack.10), calls=%async_computation | async-start | bytes 1048576 | tf_op jit(solution)/shard_map/all_to_all | solution.py:18
  17.4 13.9 %copy-start.2 = (f32[8192]{0:T(1024)S(1)}, f32[8192]{0:T(1024)}, u32[]{:S(2)}) copy-start(f32[8192]{0:T(1024)} %param.17) | copy-start | bytes 98308
  31.2 148.5 %copy-start.3 = (s32[2,2048]{1,0:T(2,128)S(1)}, s32[2,2048]{1,0:T(2,128)}, u32[]{:S(2)}) copy-start(s32[2,2048]{1,0:T(2,128)} %param.20) | copy-start | bytes 49156
  31.2 163.1 %copy-start.4 = (s32[2048]{0:T(1024)S(1)}, s32[2048]{0:T(1024)}, u32[]{:S(2)}) copy-start(s32[2048]{0:T(1024)} %param.19) | copy-start | bytes 24580
  31.2 163.1 %copy-start.1 = (f32[4096]{0:T(1024)S(1)}, f32[4096]{0:T(1024)}, u32[]{:S(2)}) copy-start(f32[4096]{0:T(1024)} %param.16) | copy-start | bytes 49156
  173.0 13.1 %all-to-all-start.1 = ((f32[16,1,512]{2,1,0:T(1,128)}), f32[16,1,512]{2,1,0:T(1,128)S(1)}, u32[]{:S(2)}, u32[]{:S(2)}) async-start(f32[16,1,512]{2,1,0:T(1,128)} %broadcast_in_dim.72), calls=%async_computation.1 | async-start | bytes 65536 | tf_op jit(solution)/shard_map/all_to_all | solution.py:31
  187.2 54.4 %all-to-all-start.2 = ((f32[8,8192,2]{1,2,0:T(2,128)}), f32[8,8192,2]{1,2,0:T(2,128)S(1)}, u32[]{:S(2)}, u32[]{:S(2)}) async-start(f32[8,8192,2]{1,2,0:T(2,128)} %stack.11), calls=%async_computation.2 | async-start | bytes 1048576 | tf_op jit(solution)/shard_map/all_to_all | solution.py:18
  194.3 335.5 %all-reduce.3.cloned.1.call-start = ((), (), s32[]{:S(2)}) async-start(), calls=%async_computation.3 | async-start | bytes 25165824
  241.9 23.7 %copy-start = (f32[4096]{0:T(1024)S(1)}, f32[4096]{0:T(1024)}, u32[]{:S(2)}) copy-start(f32[4096]{0:T(1024)} %param.15) | copy-start | bytes 49156
  253.8 55.2 %slice-start = ((s8[6291456]{0:T(1024)(128)(4,1)}), s8[2097152]{0:T(1024)(128)(4,1)S(1)}, s32[]{:S(2)}) async-start(s8[6291456]{0:T(1024)(128)(4,1)} %bitcast.106), calls=%async_computation.4 | async-start | bytes 4194304
  294.1 14.9 %slice-start.1 = ((s8[6291456]{0:T(1024)(128)(4,1)}), s8[4194304]{0:T(1024)(128)(4,1)S(1)}, s32[]{:S(2)}) async-start(s8[6291456]{0:T(1024)(128)(4,1)} %bitcast.106), calls=%async_computation.5 | async-start | bytes 8388608
  350.6 0.7 copy-start.5
Sparse Core Ops, SparseCore 0:
  350.7 178.9 all-reduce.2
